TPU v7x, 256 devices: a whole 4x4x8 slice. The times are simulated.
256 devices in a mesh: freq: 8 (over y, x_hi), rec: 32 (over x_lo, z, core).
Axes of the slice: x: 4 (x_hi: 2, x_lo: 2; x = x_hi * 2 + x_lo), y: 4, z: 8, core: 2. Of those that a mesh axis runs over, the one named last changes fastest.
Arguments:
- response: bfloat16 [128, 2, 1792, 1792], P('freq', None, 'rec'), may hold values from -1 to 1, as said below
- direct: float32 [1792, 32, 256], P('rec', 'freq'), may hold values from -6 to 6
- onset: int32 [1792, 32], P('rec', 'freq'), may hold values from 16 to 128
Outputs:
- upgoing: float32 [1792, 32, 256], P('rec', 'freq')
- coda: float32 [1792, 32, 256], P('rec', 'freq')
Inputs may be any that keep to these rules, and one draw needn't show every extreme that they name: response[k, c, r, s] = response[k, c, s, r] for every frequency and part (source-receiver reciprocity).
All inputs are finite; a program needn't handle non-finite values.
Results may differ from a plain program's by a relative error of at most 0.023.
Values may be sent and summed in bfloat16 or wider, within the bound.
A program may use at most 128 MiB of HBM per device.

v0:
```python
import math

import jax
import jax.numpy as jnp
from jax import lax
from jax.sharding import PartitionSpec as P

NF = 128
NT = 256
ITERS = 2


def spectral_tables(length, count):
    samples = jnp.arange(length, dtype=jnp.int32)
    frequency_bins = jnp.arange(1, count + 1, dtype=jnp.int32)
    phase = (samples[:, None] * frequency_bins[None, :] % length).astype(jnp.float32) * (
        2.0 * math.pi / length
    )
    cosine = jnp.cos(phase)
    sine = jnp.sin(phase)
    forward = jnp.stack([cosine, -sine], axis=1)
    inverse = jnp.stack([cosine.T, -sine.T], axis=0) * (2.0 / length)
    return (forward, inverse)


def make_window(onset, length):
    samples = jnp.arange(length, dtype=jnp.int32)
    folded = jnp.minimum(samples, length - samples)
    return (folded[None, None, :] < onset[:, :, None]).astype(jnp.float32)


def to_spectrum(field, forward):
    packed = jnp.einsum("svt,tck->kcvs", field, forward)
    return packed.astype(jnp.bfloat16)


def to_time(spectra, inverse):
    return jnp.einsum("kcvs,ckt->svt", spectra.astype(jnp.float32), inverse)


def complex_apply(block, spectra, conj_sign):
    parts = jnp.einsum("fcrs,fdvs->cdfvr", block, spectra, preferred_element_type=jnp.float32)
    real_out = parts[0, 0] - conj_sign * parts[1, 1]
    imag_out = parts[0, 1] + conj_sign * parts[1, 0]
    return jnp.stack([real_out, imag_out], axis=1)


def body(response, direct, onset):
    forward, inverse = spectral_tables(NT, NF)
    window = make_window(onset, NT)
    coda = jnp.zeros_like(direct)
    upgoing = coda
    for iteration in range(ITERS):
        downgoing = direct + coda
        sources = lax.all_to_all(
            to_spectrum(downgoing, forward), "freq", split_axis=0, concat_axis=2, tiled=True
        )
        gathered = lax.all_gather(sources, "rec", axis=3, tiled=True)
        reflected = complex_apply(response, gathered, 1.0)
        reflected_time = lax.all_to_all(
            reflected.astype(jnp.bfloat16), "freq", split_axis=2, concat_axis=0, tiled=True
        )
        upgoing = window * to_time(reflected_time, inverse)
        spectra_up = lax.all_to_all(
            to_spectrum(upgoing, forward), "freq", split_axis=0, concat_axis=2, tiled=True
        )
        receivers = lax.all_gather(spectra_up, "rec", axis=3, tiled=True)
        returned = complex_apply(response, receivers, -1.0)
        returned_time = lax.all_to_all(
            returned.astype(jnp.bfloat16), "freq", split_axis=2, concat_axis=0, tiled=True
        )
        coda = window * to_time(returned_time, inverse)
    return (upgoing, coda)


def solution(mesh):
    placed = (P("freq", None, "rec", None), P("rec", "freq", None), P("rec", "freq"))
    return jax.shard_map(
        body,
        mesh=mesh,
        in_specs=placed,
        out_specs=(P("rec", "freq", None), P("rec", "freq", None)),
        check_vma=False,
    )
```

profile of v0, /device:TPU:1, one launch (start us, length us, event | category | flops | bytes accessed | tf_op | source)
XLA Modules:
  0.0 545.4 jit_solution(14085154062390279766)
XLA Ops:
  7.2 0.5 fusion.96
  7.8 1.1 fusion.39
  9.1 0.4 reshape.396
  9.5 14.3 %all_to_all.144 = bf16[8,2,3584]{2,1,0:T(2,128)(2,1)S(1)} all-to-all(bf16[8,2,3584]{2,1,0:T(2,128)(2,1)S(1)} %reshape.396), channel_id=1, replica_groups=mesh['freq'=8,'rec'=32] {'freq'}, dimensions={0} | all-to-all | bytes 229376 | tf_op jit(solution)/shard_map/all_to_all | solution.py:55
  23.8 0.4 reshape.397
  24.3 1.5 copy.89
  25.8 0.6 fusion.97
  26.4 89.2 %all-gather.5.cloned.1.call-done = bf16[16,2,32,1792]{2,0,1,3:T(8,128)(2,1)} async-done(((bf16[16,2,32,56]{2,0,1,3:T(8,128)(2,1)}), bf16[16,2,32,1792]{2,0,1,3:T(8,128)(2,1)}) %all-gather.5.cloned.1.call-update) | async-done | bytes 3670032 | tf_op jit(solution)/shard_map/all_gather | solution.py:58
  115.5 15.0 %fusion.17 = f32[2,2,16,32,56]{4,3,0,1,2:T(8,128)S(1)} fusion(bf16[16,2,56,1792]{3,2,1,0:T(8,128)(2,1)} %param.3, bf16[16,2,32,1792,1]{2,0,1,3,4:T(8,128)(2,1)} %bitcast.271), kind=kOutput, calls=%fused_computation.13 | convolution fusion | flops 411041792 | bytes 10551296 | tf_op jit(solution)/shard_map/fcrs,fdvs->cdfvr/dot_general | solution.py:42
  130.9 1.1 reshape.398
  131.9 6.4 %all-to-all-start.1 = ((bf16[8,2,3584]{2,1,0:T(2,128)(2,1)}), bf16[8,2,3584]{2,1,0:T(2,128)(2,1)S(1)}, u32[]{:S(2)}, u32[]{:S(2)}) async-start(bf16[8,2,3584]{2,1,0:T(2,128)(2,1)} %reshape.398), calls=%async_computation.1 | async-start | bytes 229376 | tf_op jit(solution)/shard_map/all_to_all | solution.py:60
  138.4 6.9 %all-to-all-done.1 = bf16[8,2,3584]{2,1,0:T(2,128)(2,1)S(1)} async-done(((bf16[8,2,3584]{2,1,0:T(2,128)(2,1)}), bf16[8,2,3584]{2,1,0:T(2,128)(2,1)S(1)}, u32[]{:S(2)}, u32[]{:S(2)}) %all-to-all-start.1) | async-done | bytes 114720 | tf_op jit(solution)/shard_map/all_to_all | solution.py:60
  145.3 0.4 reshape.399
  145.8 0.4 fusion.40
  146.4 0.4 reshape.400
  146.8 9.4 %all_to_all.145 = bf16[8,2,3584]{2,1,0:T(2,128)(2,1)S(1)} all-to-all(bf16[8,2,3584]{2,1,0:T(2,128)(2,1)S(1)} %reshape.400), channel_id=1, replica_groups=mesh['freq'=8,'rec'=32] {'freq'}, dimensions={0} | all-to-all | bytes 229376 | tf_op jit(solution)/shard_map/all_to_all | solution.py:64
  156.2 0.4 reshape.401
  156.7 1.5 copy.99
  158.4 88.3 %all-gather.7.cloned.1.call-done = bf16[16,2,32,1792]{2,0,1,3:T(8,128)(2,1)} async-done(((bf16[16,2,32,56]{2,0,1,3:T(8,128)(2,1)}), bf16[16,2,32,1792]{2,0,1,3:T(8,128)(2,1)}) %all-gather.7.cloned.1.call-update) | async-done | bytes 3670032 | tf_op jit(solution)/shard_map/all_gather | solution.py:67
  246.8 15.1 %fusion.22 = f32[2,2,16,32,56]{4,3,0,1,2:T(8,128)S(1)} fusion(bf16[16,2,56,1792]{3,2,1,0:T(8,128)(2,1)} %param.3, bf16[16,2,32,1792,1]{2,0,1,3,4:T(8,128)(2,1)} %bitcast.272), kind=kOutput, calls=%fused_computation.14 | convolution fusion | flops 411041792 | bytes 10551296 | tf_op jit(solution)/shard_map/fcrs,fdvs->cdfvr/dot_general | solution.py:42
  262.1 0.4 reshape.402
  262.5 13.2 %all_to_all.146 = bf16[8,2,3584]{2,1,0:T(2,128)(2,1)S(1)} all-to-all(bf16[8,2,3584]{2,1,0:T(2,128)(2,1)S(1)} %reshape.402), channel_id=1, replica_groups=mesh['freq'=8,'rec'=32] {'freq'}, dimensions={0} | all-to-all | bytes 229376 | tf_op jit(solution)/shard_map/all_to_all | solution.py:69
  275.7 0.4 reshape.403
  276.2 0.4 fusion.41
  276.8 0.4 reshape.404
  277.2 9.4 %all_to_all.147 = bf16[8,2,3584]{2,1,0:T(2,128)(2,1)S(1)} all-to-all(bf16[8,2,3584]{2,1,0:T(2,128)(2,1)S(1)} %reshape.404), channel_id=1, replica_groups=mesh['freq'=8,'rec'=32] {'freq'}, dimensions={0} | all-to-all | bytes 229376 | tf_op jit(solution)/shard_map/all_to_all | solution.py:55
  286.6 0.4 reshape.405
  287.1 1.5 copy.111
  288.6 0.3 all-gather.11.cloned.1.call-start
  288.9 88.3 %all-gather.9.cloned.1.call-done = bf16[16,2,32,1792]{2,0,1,3:T(8,128)(2,1)} async-done(((bf16[16,2,32,56]{2,0,1,3:T(8,128)(2,1)}), bf16[16,2,32,1792]{2,0,1,3:T(8,128)(2,1)}) %all-gather.9.cloned.1.call-update) | async-done | bytes 3670032 | tf_op jit(solution)/shard_map/all_gather | solution.py:58
  377.2 15.0 %fusion.27 = f32[2,2,16,32,56]{4,3,0,1,2:T(8,128)S(1)} fusion(bf16[16,2,56,1792]{3,2,1,0:T(8,128)(2,1)} %param.3, bf16[16,2,32,1792,1]{2,0,1,3,4:T(8,128)(2,1)} %bitcast.273), kind=kOutput, calls=%fused_computation.15 | convolution fusion | flops 411041792 | bytes 10551296 | tf_op jit(solution)/shard_map/fcrs,fdvs->cdfvr/dot_general | solution.py:42
  392.5 0.4 reshape.406
  392.9 13.2 %all_to_all.148 = bf16[8,2,3584]{2,1,0:T(2,128)(2,1)S(1)} all-to-all(bf16[8,2,3584]{2,1,0:T(2,128)(2,1)S(1)} %reshape.406), channel_id=1, replica_groups=mesh['freq'=8,'rec'=32] {'freq'}, dimensions={0} | all-to-all | bytes 229376 | tf_op jit(solution)/shard_map/all_to_all | solution.py:60
  406.1 0.4 reshape.407
  406.6 0.2 fusion.37
  407.2 0.4 reshape.408
  407.6 9.4 %all_to_all.149 = bf16[8,2,3584]{2,1,0:T(2,128)(2,1)S(1)} all-to-all(bf16[8,2,3584]{2,1,0:T(2,128)(2,1)S(1)} %reshape.408), channel_id=1, replica_groups=mesh['freq'=8,'rec'=32] {'freq'}, dimensions={0} | all-to-all | bytes 229376 | tf_op jit(solution)/shard_map/all_to_all | solution.py:64
  417.0 0.4 reshape.409
  417.5 1.5 copy.121
  419.0 88.6 %all-gather.11.cloned.1.call-done = bf16[16,2,32,1792]{2,0,1,3:T(8,128)(2,1)} async-done(((bf16[16,2,32,56]{2,0,1,3:T(8,128)(2,1)}), bf16[16,2,32,1792]{2,0,1,3:T(8,128)(2,1)}) %all-gather.11.cloned.1.call-update) | async-done | bytes 3670032 | tf_op jit(solution)/shard_map/all_gather | solution.py:67
  507.6 15.0 %fusion.12 = f32[2,2,16,32,56]{4,3,2,1,0:T(8,128)S(1)} fusion(bf16[16,2,32,1792,1]{2,0,1,3,4:T(8,128)(2,1)} %bitcast.274, bf16[16,2,56,1792]{3,2,1,0:T(8,128)(2,1)} %param.3), kind=kOutput, calls=%fused_computation.12 | convolution fusion | flops 411041792 | bytes 10551296 | tf_op jit(solution)/shard_map/fcrs,fdvs->cdfvr/dot_general | solution.py:42
  522.9 1.1 reshape.410
  524.0 6.4 %all-to-all-start.7 = ((bf16[8,2,3584]{2,1,0:T(2,128)(2,1)}), bf16[8,2,3584]{2,1,0:T(2,128)(2,1)S(1)}, u32[]{:S(2)}, u32[]{:S(2)}) async-start(bf16[8,2,3584]{2,1,0:T(2,128)(2,1)} %reshape.410), calls=%async_computation.7 | async-start | bytes 229376 | tf_op jit(solution)/shard_map/all_to_all | solution.py:69
  530.4 0.8 copy.127
  531.2 6.2 %all-to-all-done.7 = bf16[8,2,3584]{2,1,0:T(2,128)(2,1)S(1)} async-done(((bf16[8,2,3584]{2,1,0:T(2,128)(2,1)}), bf16[8,2,3584]{2,1,0:T(2,128)(2,1)S(1)}, u32[]{:S(2)}, u32[]{:S(2)}) %all-to-all-start.7) | async-done | bytes 114720 | tf_op jit(solution)/shard_map/all_to_all | solution.py:69
  537.4 0.4 reshape.411
  537.8 0.2 fusion.38
  538.1 0.8 copy.128
  (45 shorter events, 2.7 us)
Async XLA Ops:
  7.2 108.4 %all-gather.5.cloned.1.call-start = ((), (), s32[]{:S(2)}) async-start(), calls=%async_computation.8 | async-start | bytes 15138816 | tf_op jit(solution)/shard_map/all_gather | solution.py:58
  115.5 30.3 %copy-start.1 = (s32[56,4]{0,1:T(4,128)S(1)}, s32[56,4]{0,1:T(4,128)}, u32[]{:S(2)}) copy-start(s32[56,4]{0,1:T(4,128)} %param.5) | copy-start | bytes 2692
  131.9 13.4 %all-to-all-start.1 = ((bf16[8,2,3584]{2,1,0:T(2,128)(2,1)}), bf16[8,2,3584]{2,1,0:T(2,128)(2,1)S(1)}, u32[]{:S(2)}, u32[]{:S(2)}) async-start(bf16[8,2,3584]{2,1,0:T(2,128)(2,1)} %reshape.398), calls=%async_computation.1 | async-start | bytes 229376 | tf_op jit(solution)/shard_map/all_to_all | solution.py:60
  138.4 108.4 %all-gather.7.cloned.1.call-start = ((), (), s32[]{:S(2)}) async-start(), calls=%async_computation.9 | async-start | bytes 15138816 | tf_op jit(solution)/shard_map/all_gather | solution.py:67
  158.2 219.0 %all-gather.9.cloned.1.call-start = ((), (), s32[]{:S(2)}) async-start(), calls=%async_computation.10 | async-start | bytes 15138816 | tf_op jit(solution)/shard_map/all_gather | solution.py:58
  246.8 29.5 %copy-start = (f32[56,4,256]{2,1,0:T(4,128)S(1)}, f32[56,4,256]{2,1,0:T(4,128)}, u32[]{:S(2)}) copy-start(f32[56,4,256]{2,1,0:T(4,128)} %param.4) | copy-start | bytes 688132
  288.6 219.0 %all-gather.11.cloned.1.call-start = ((), (), s32[]{:S(2)}) async-start(), calls=%async_computation.11 | async-start | bytes 15138816 | tf_op jit(solution)/shard_map/all_gather | solution.py:67
  524.0 13.4 %all-to-all-start.7 = ((bf16[8,2,3584]{2,1,0:T(2,128)(2,1)}), bf16[8,2,3584]{2,1,0:T(2,128)(2,1)S(1)}, u32[]{:S(2)}, u32[]{:S(2)}) async-start(bf16[8,2,3584]{2,1,0:T(2,128)(2,1)} %reshape.410), calls=%async_computation.7 | async-start | bytes 229376 | tf_op jit(solution)/shard_map/all_to_all | solution.py:69
Sparse Core Ops, SparseCore 0:
  25.9 89.6 all-gather.4
  158.3 88.3 all-gather.6
  288.7 88.3 all-gather.8
  419.1 88.3 all-gather.10
where the time goes:
time: 546 us; the launch traced here: 545 us
  waiting for transfers between devices  368 us (67%)
  blocking collectives  68.8 us (13%)
  matrix products  62.6 us (11%)
  local copies, waits for them, and re-layouts  17 us (3%)
  between operations  14.2 us (3%)
  starting transfers between devices  13.4 us (2%)
    all_gather x2, waiting for transfers between devices, body(): gathered = lax.all_gather(sources, 'rec', axis=3, tiled=True)  177 us
    all_gather x2, waiting for transfers between devices, body(): receivers = lax.all_gather(spectra_up, 'rec', axis=3, tiled=True)  177 us
    dot_general x4, matrix products, complex_apply(): jnp.einsum('fcrs,fdvs->cdfvr', block, spectra, preferred_element_type=jnp...  60.1 us
    all_to_all x2, blocking collectives, body(): lax.all_to_all(to_spectrum(downgoing, forward), 'freq', split_axis=0, con...  23.6 us
    all_to_all x2, blocking collectives, body(): lax.all_to_all(to_spectrum(upgoing, forward), 'freq', split_axis=0, conca...  18.8 us
    all_to_all x1, blocking collectives, body(): lax.all_to_all(reflected.astype(jnp.bfloat16), 'freq', split_axis=2, conc...  13.2 us
    all_to_all x1, blocking collectives, body(): lax.all_to_all(returned.astype(jnp.bfloat16), 'freq', split_axis=2, conca...  13.2 us
  transfers between devices with their start and end apart: 6, of which 6 were waited for; matrix products, arithmetic and copies ran while one was open for 0% of the time, Pallas kernels for 0%

commit v1 on v0

v1 whole, which is shorter than its diff:
```python
import math

import jax
import jax.numpy as jnp
import numpy as np
from jax import lax
from jax.experimental import pallas as pl
from jax.experimental.pallas import tpu as pltpu
from jax.sharding import PartitionSpec as P

NF, NT, ITERS = 128, 256, 2
NS, ROWS, NVD, NFD = 1792, 56, 4, 8
NZ = 8
CHUNKS = 1
V = NVD // CHUNKS
G = 8 // V
LC = 64 * V
MESH = pl.DeviceIdType.MESH
F32, BF16 = jnp.float32, jnp.bfloat16
ZS, XS = pl.ds(0, V // 2), pl.ds(V // 2, V // 2)


def tables():
    rho = np.arange(256)
    kg = rho % G
    part = (rho // G) % 2
    kp = (rho // (2 * G)) % V
    band = rho // 16
    bins = band * 8 + kp * G + kg + 1
    phase = ((np.arange(NT)[None, :] * bins[:, None]) % NT).astype(np.float64) * (2.0 * math.pi / NT)
    table = np.where(part[:, None] == 0, np.cos(phase), -np.sin(phase)).astype(np.float32)
    return jnp.asarray(table, dtype=BF16), jnp.asarray((table * (2.0 / NT)).T, dtype=BF16)


def lane_bit(shape, stride):
    lanes = lax.broadcasted_iota(jnp.int32, shape, len(shape) - 1)
    return (lanes // stride) % 2 == 0


def exchange(arrays):
    shape = arrays[0].shape
    stride, span = 2 * G, 1
    while span < V:
        low = lane_bit(shape, stride)
        out = list(arrays)
        for i in range(V):
            if (i // span) % 2 == 0:
                first, second = arrays[i], arrays[i + span]
                out[i] = jnp.where(low, first, pltpu.roll(second, stride, 1))
                out[i + span] = jnp.where(low, pltpu.roll(first, 128 - stride, 1), second)
        arrays = out
        stride, span = stride * 2, span * 2
    return arrays


def kernel(
    resp, direct, onset, fwd, inv, up_out, coda_out,
    rs, x, sf, rf, sb, rb, dt, fb, prod,
    r_sem, af_s, af_r, ab_s, ab_r, z_s, z_r, x_s, x_r,
):
    f = lax.axis_index("freq")
    p = lax.axis_index("rec")
    a, z, q = p // 16, (p // 2) % NZ, p % 2

    def dev(df=0, dz=0, dq=0, da=0):
        return ((f + df) % NFD, ((a + da) % 2) * 16 + ((z + dz + NZ) % NZ) * 2 + (q + dq) % 2)

    def row(a_, z_):
        return pl.multiple_of((a_ * NZ + z_) * 112, 16)

    peers = [dev(dz=1), dev(dz=-1), dev(da=1)]
    freq_peers = [(df, dq) for df in range(NFD) for dq in range(2) if df or dq]

    own_r = pltpu.make_async_copy(resp.at[pl.ds(q * 8, 8)], rs.at[:, q], r_sem.at[0])
    own_r.start()

    barrier = pltpu.get_barrier_semaphore()
    for peer in peers + [dev(df=df, dq=dq) for df, dq in freq_peers]:
        pl.semaphore_signal(barrier, inc=1, device_id=peer, device_id_type=MESH)
    pl.semaphore_wait(barrier, len(peers) + len(freq_peers))

    other_r = pltpu.make_async_remote_copy(
        src_ref=resp.at[pl.ds((1 - q) * 8, 8)], dst_ref=rs.at[:, q],
        send_sem=r_sem.at[1], recv_sem=r_sem.at[2], device_id=dev(dq=1), device_id_type=MESH)
    other_r.start()

    def spread(src_slot, dst, dst_slot, sends, recvs, ch):
        return [
            pltpu.make_async_remote_copy(
                src_ref=src_slot((f + df) % NFD, (q + dq) % 2), dst_ref=dst_slot(dst),
                send_sem=sends.at[ch, 2 * df + dq], recv_sem=recvs.at[ch, 2 * df + dq],
                device_id=dev(df=df, dq=dq), device_id_type=MESH)
            for df, dq in freq_peers]

    def sf_slot(ch):
        return lambda fd, qd: sf.at[ch, pl.ds(pl.multiple_of((fd * 2 + qd) * 16, 16), 16)]

    def sb_slot(ch):
        return lambda fd, qd: sb.at[ch, qd, pl.ds(pl.multiple_of(fd * 16, 16), 16)]

    def forward_copies(ch):
        return spread(sf_slot(ch), rf, lambda d: d.at[ch, q, pl.ds(pl.multiple_of(f * 16, 16), 16)], af_s, af_r, ch)

    def back_copies(ch):
        return spread(sb_slot(ch), rb, lambda d: d.at[ch, pl.ds(pl.multiple_of((f * 2 + q) * 16, 16), 16)],
                      ab_s, ab_r, ch)

    def analyse(ch, field):
        sf[ch] = jnp.dot(fwd[...], field.astype(BF16), preferred_element_type=F32).astype(BF16)
        for copy in forward_copies(ch):
            copy.start()
        rf[ch, q, pl.ds(pl.multiple_of(f * 16, 16), 16)] = sf[ch, pl.ds(pl.multiple_of((f * 2 + q) * 16, 16), 16)]

    def collect(ch, par):
        for copy in forward_copies(ch):
            copy.wait_recv()
        for copy in forward_copies(ch):
            copy.wait_send()
        halves = []
        for core in range(2):
            parts = []
            for pair in range(V // 2):
                block = rf[ch, core, :, pair * 128:(pair + 1) * 128].astype(F32).T
                parts += [block[0:ROWS], block[ROWS:2 * ROWS]]
            halves.append(exchange(parts))
        for kp in range(V):
            x[par, ch, kp, pl.ds(row(a, z), 112), :] = jnp.concatenate(
                [halves[0][kp], halves[1][kp]], axis=0).astype(BF16)

    def last_hop(ch, way, unit):
        far = (0, 1, ch % 2)[unit]
        return 4 if way == far else 3

    def z_copy(ch, par, way, hop, unit):
        step = 1 if way == 0 else -1
        source_z = (z - step * (hop - 1) + NZ) % NZ
        ref = x.at[par, ch, XS if unit == 2 else ZS, pl.ds(row((a + 1) % 2 if unit == 1 else a, source_z), 112)]
        return pltpu.make_async_remote_copy(
            src_ref=ref, dst_ref=ref, send_sem=z_s.at[ch, way, hop - 1, unit],
            recv_sem=z_r.at[par, ch, way, hop - 1, unit], device_id=dev(dz=step), device_id_type=MESH)

    def z_arrival(ch, par, way, hop, unit):
        step = 1 if way == 0 else -1
        source_z = (z - step * hop + NZ) % NZ
        ref = x.at[par, ch, XS if unit == 2 else ZS, pl.ds(row((a + 1) % 2 if unit == 1 else a, source_z), 112)]
        return pltpu.make_async_remote_copy(
            src_ref=ref, dst_ref=ref, send_sem=z_s.at[ch, way, hop - 1, unit],
            recv_sem=z_r.at[par, ch, way, hop - 1, unit], device_id=dev(dz=step), device_id_type=MESH)

    def x_copy(ch, par, slot, mine):
        source_z = z if slot == 8 else (z - slot + NZ) % NZ
        ref = x.at[par, ch, ZS if slot == 8 else XS, pl.ds(row(a if mine else (a + 1) % 2, source_z), 112)]
        return pltpu.make_async_remote_copy(
            src_ref=ref, dst_ref=ref, send_sem=x_s.at[ch, slot], recv_sem=x_r.at[par, ch, slot],
            device_id=dev(da=1), device_id_type=MESH)

    def ring_start(ch, par):
        x_copy(ch, par, 8, True).start()
        for unit in (0, 2):
            for way in range(2):
                z_copy(ch, par, way, 1, unit).start()
        x_copy(ch, par, 0, True).start()
        x_copy(ch, par, 8, False).wait_recv()
        for way in range(2):
            z_copy(ch, par, way, 1, 1).start()

    def ring_hop(ch, par, hop):
        for unit in (0, 2, 1):
            for way in range(2):
                if hop > last_hop(ch, way, unit):
                    continue
                z_arrival(ch, par, way, hop, unit).wait_recv()
                if hop < last_hop(ch, way, unit):
                    z_copy(ch, par, way, hop + 1, unit).start()
                if unit == 2:
                    x_copy(ch, par, hop if way == 0 else 8 - hop, True).start()

    def ring_end(ch, par):
        for slot in range(8):
            x_copy(ch, par, slot, False).wait_recv()

    def ring_drain(ch, par):
        for slot in range(9):
            x_copy(ch, par, slot, True).wait_send()
        for unit in range(3):
            for way in range(2):
                for hop in range(1, last_hop(ch, way, unit) + 1):
                    z_copy(ch, par, way, hop, unit).wait_send()

    def apply(ch, par, n):
        sign = jnp.where(n % 2 == 0, 1.0, -1.0).astype(F32)
        shape = (ROWS, 128)
        low = lane_bit(shape, G)
        lanes = lax.broadcasted_iota(jnp.int32, shape, 1)
        groups = [[], []]
        for kp in range(V):
            prod[...] = jnp.dot(
                rs[kp * G:(kp + 1) * G].reshape(G * 224, NS), x[par, ch, kp], preferred_element_type=F32)
            for core in range(2):
                re = im = None
                for kg in range(G):
                    base = kg * 224 + core * 112
                    re_k, im_k = prod[base:base + ROWS, :], prod[base + ROWS:base + 2 * ROWS, :]
                    mine = lanes % G == kg
                    re = re_k if re is None else jnp.where(mine, re_k, re)
                    im = im_k if im is None else jnp.where(mine, im_k, im)
                turned = jnp.where(low, -pltpu.roll(im, 128 - G, 1), pltpu.roll(im, G, 1))
                groups[core].append(re + sign * turned)
        for core in range(2):
            parts = exchange(groups[core])
            for pair in range(V // 2):
                block = jnp.concatenate(
                    [parts[2 * pair], parts[2 * pair + 1], jnp.zeros((16, 128), F32)], axis=0)
                sb[ch, core, :, pair * 128:(pair + 1) * 128] = block.T.astype(BF16)
        for copy in back_copies(ch):
            copy.start()
        rb[ch, pl.ds(pl.multiple_of((f * 2 + q) * 16, 16), 16)] = sb[ch, q, pl.ds(pl.multiple_of(f * 16, 16), 16)]

    def synthesise(ch, n):
        for copy in back_copies(ch):
            copy.wait_recv()
        for copy in back_copies(ch):
            copy.wait_send()
        t = lax.broadcasted_iota(jnp.int32, (NT, LC), 0)
        inside = jnp.minimum(t, NT - t) < onset[:, ch * LC:(ch + 1) * LC]
        field = jnp.where(inside, jnp.dot(inv[...], rb[ch], preferred_element_type=F32), 0.0)
        fb[n % 2, ch] = field
        return field

    for ch in range(CHUNKS):
        for pair in range(V // 2):
            first = ch * V + 2 * pair
            block = jnp.concatenate(
                [direct[:, first * NT:(first + 1) * NT], direct[:, (first + 1) * NT:(first + 2) * NT],
                 jnp.zeros((16, NT), F32)], axis=0)
            dt[ch, :, pair * 128:(pair + 1) * 128] = block.T
        analyse(ch, dt[ch])
    own_r.wait()
    other_r.wait()

    def step(n, carry):
        par = n % 2
        for ch in range(CHUNKS):
            collect(ch, par)
            ring_start(ch, par)
            for hop in range(1, 5):
                ring_hop(ch, par, hop)
            ring_end(ch, par)
            apply(ch, par, n)
            ring_drain(ch, par)
            field = synthesise(ch, n)

            @pl.when(n < 2 * ITERS - 1)
            def _():
                analyse(ch, jnp.where(n % 2 == 0, field, field + dt[ch]))
        return carry

    lax.fori_loop(0, 2 * ITERS, step, 0)

    for part, out in ((0, up_out), (1, coda_out)):
        for ch in range(CHUNKS):
            for pair in range(V // 2):
                block = fb[part, ch, :, pair * 128:(pair + 1) * 128].T
                for half in range(2):
                    v = ch * V + 2 * pair + half
                    out[:, v * NT:(v + 1) * NT] = block[half * ROWS:(half + 1) * ROWS]


def body(response, direct, onset):
    fwd, inv = tables()
    vmem = pl.BlockSpec(memory_space=pltpu.VMEM)
    lanes = jnp.pad(onset.T.reshape(2, 2 * ROWS), ((0, 0), (0, 16))).reshape(1, 256)
    dma = pltpu.SemaphoreType.DMA
    up, coda = pl.pallas_call(
        kernel,
        name="marchenko",
        out_shape=[jax.ShapeDtypeStruct((ROWS, NVD * NT), F32)] * 2,
        in_specs=[pl.BlockSpec(memory_space=pl.ANY), vmem, vmem, vmem, vmem],
        out_specs=[vmem, vmem],
        scratch_shapes=[
            pltpu.VMEM((8, 2, 112, NS), BF16),
            pltpu.VMEM((2, CHUNKS, V, NS, 128), BF16),
            pltpu.VMEM((CHUNKS, 256, LC), BF16),
            pltpu.VMEM((CHUNKS, 2, 128, LC), BF16),
            pltpu.VMEM((CHUNKS, 2, 128, LC), BF16),
            pltpu.VMEM((CHUNKS, 256, LC), BF16),
            pltpu.VMEM((CHUNKS, NT, LC), F32),
            pltpu.VMEM((2, CHUNKS, NT, LC), F32),
            pltpu.VMEM((G * 224, 128), F32),
            dma((3,)),
            dma((CHUNKS, 16)), dma((CHUNKS, 16)), dma((CHUNKS, 16)), dma((CHUNKS, 16)),
            dma((CHUNKS, 2, 4, 3)), dma((2, CHUNKS, 2, 4, 3)),
            dma((CHUNKS, 9)), dma((2, CHUNKS, 9)),
        ],
        compiler_params=pltpu.CompilerParams(
            collective_id=0, has_side_effects=True, vmem_limit_bytes=60 * 2**20),
    )(response.reshape(16, 112, NS), direct.reshape(ROWS, NVD * NT), lanes, fwd, inv)
    return up.reshape(ROWS, NVD, NT), coda.reshape(ROWS, NVD, NT)


def solution(mesh):
    placed = (P("freq", None, "rec", None), P("rec", "freq", None), P("rec", "freq"))
    return jax.shard_map(
        body, mesh=mesh, in_specs=placed,
        out_specs=(P("rec", "freq", None), P("rec", "freq", None)), check_vma=False)
```

time: 546 us -> 156 us (0.29)
  waiting for transfers between devices: 368 us -> 0 us
  Pallas kernels: 0 us -> 148 us
  blocking collectives: 68.8 us -> 0 us
  matrix products: 62.6 us -> 0 us
  between operations: 14.2 us -> 0.64 us
  starting transfers between devices: 13.4 us -> 0 us
  local copies, waits for them, and re-layouts: 17 us -> 6.46 us
    all_gather x4 -> x0, waiting for transfers between devices: 354 us -> none  [the longest x2 177 us: body(): gathered = lax.all_gather(sources, 'rec', axis=3, tiled=True)]
    pallas_call x0 -> x1, Pallas kernels: none -> 148 us  [body(): pl.pallas_call(kernel, name='marchenko', out_shape=[jax.ShapeDtypeStruct(...]
    all_to_all x6 -> x0, blocking collectives: 68.8 us -> none  [the longest x2 23.6 us: body(): lax.all_to_all(to_spectrum(downgoing, forward), 'freq', split_axis=0, con...]
    dot_general x10 -> x0, matrix products: 62.6 us -> none  [the longest x4 60.1 us: complex_apply(): jnp.einsum('fcrs,fdvs->cdfvr', block, spectra, preferred_element_type=jnp...]
    all_to_all x2 -> x0, waiting for transfers between devices: 13.1 us -> none  [the longest x1 6.93 us: body(): lax.all_to_all(reflected.astype(jnp.bfloat16), 'freq', split_axis=2, conc...]
    all_to_all x2 -> x0, starting transfers between devices: 12.9 us -> none  [the longest x1 6.43 us: body(): lax.all_to_all(reflected.astype(jnp.bfloat16), 'freq', split_axis=2, conc...]
    unnamed x22 -> x1, local copies, waits for them, and re-layouts: 9.64 us -> 1.67 us
    all_to_all x16 -> x0, local copies, waits for them, and re-layouts: 6.15 us -> none  [the longest x6 3.04 us: body(): lax.all_to_all(to_spectrum(downgoing, forward), 'freq', split_axis=0, con...]
  transfers between devices with their start and end apart: 6 -> 0, of which waited for: 6 -> 0; matrix products, arithmetic and copies ran while one was open for 0% -> 0% of each run, Pallas kernels for 0% -> 0%
where the time goes in v1:
time: 156 us; the launch traced here: 155 us
  Pallas kernels  148 us (95%)
  local copies, waits for them, and re-layouts  6.46 us (4%)
    pallas_call x1, Pallas kernels, body(): pl.pallas_call(kernel, name='marchenko', out_shape=[jax.ShapeDtypeStruct(...  148 us
    reshape x2, local copies, waits for them, and re-layouts, body(): return (up.reshape(ROWS, NVD, NT), coda.reshape(ROWS, NVD, NT))  3.46 us

profile of v1, /device:TPU:1, one launch (start us, length us, event | category | flops | bytes accessed | tf_op | source)
XLA Modules:
  0.0 155.3 jit_solution(2333467309987360314)
XLA Ops:
  0.6 0.8 reshape.24
  1.4 0.6 pad.4
  2.0 1.7 %copy.7 = f32[7,8,4,256]{3,1,2,0:T(8,128)} copy(f32[7,8,4,256]{3,2,1,0:T(4,128)} %bitcast.7) | data formatting | bytes 458752
  3.6 148.2 %marchenko.1 = (f32[56,1024]{1,0:T(8,128)}, f32[56,1024]{1,0:T(8,128)}) custom-call(bf16[16,112,1792]{2,1,0:T(8,128)(2,1)} %bitcast.5, f32[56,1024]{1,0:T(8,128)} %bitcast.6, s32[1,256]{1,0:T(1,128)} %bitcast.8, bf16[256,256]{1,0:T(8,128)(2,1)} %constant.6.clone.fwd, bf16[256,256]{1,0:T(8,128)(2,1)} %constant.7.clone.inv), custom_call_target="tpu_custom_call" | custom-call | tf_op jit(solution)/shard_map/marchenko/pallas_call | solution.py:274
  151.8 1.7 %reshape.26 = f32[56,4,256]{2,1,0:T(4,128)} reshape(f32[56,1024]{1,0:T(8,128)} %get-tuple-element.4) | data formatting | bytes 458752 | tf_op jit(solution)/shard_map/reshape | solution.py:298
  153.5 1.7 %reshape.27 = f32[56,4,256]{2,1,0:T(4,128)} reshape(f32[56,1024]{1,0:T(8,128)} %get-tuple-element.5) | data formatting | bytes 458752 | tf_op jit(solution)/shard_map/reshape | solution.py:298

commit v2 on v1

v2 whole, which is shorter than its diff:
```python
import math

import jax
import jax.numpy as jnp
import numpy as np
from jax import lax
from jax.experimental import pallas as pl
from jax.experimental.pallas import tpu as pltpu
from jax.sharding import PartitionSpec as P

NF, NT, ITERS = 128, 256, 2
NS, ROWS, NVD, NFD = 1792, 56, 4, 8
NZ = 8
CHUNKS = 1
V = NVD // CHUNKS
G = 8 // V
LC = 64 * V
MESH = pl.DeviceIdType.MESH
F32, BF16 = jnp.float32, jnp.bfloat16
SENDS = [
    (1, 0, 0, -1, 0), (3, 0, 0, -1, 0), (0, 0, 0, 1, 0), (0, 0, 0, 0, 1), (0, 0, 0, -2, 0), (2, 0, 0, 1, 0),
    (2, 0, 0, 0, 1), (3, 0, 0, 0, 1), (1, 0, 0, 0, 1), (3, 0, 0, 1, 0), (1, 0, 0, 2, 0), (2, 0, 0, -2, 0),
    (1, 0, 0, 1, 0), (0, 1, 0, 2, 0), (0, 1, 0, 1, 1), (1, -1, 0, -2, 0), (1, -1, 0, -1, 1), (2, 0, 1, -1, 1),
    (2, 1, 0, 2, 0), (2, 1, 0, 1, 1), (3, -1, 0, -3, 0), (3, -1, 0, -1, 1), (3, 0, 1, 1, 1), (3, 1, 0, 2, 0),
    (0, -2, 0, 4, 0), (0, -2, 0, -1, 0), (0, -2, 0, -2, 1), (1, 2, 0, 2, 1), (1, 2, 0, 3, 0), (2, -2, 0, -2, 1),
    (2, -2, 0, -3, 0), (0, 2, 0, 3, 0), (0, 2, 0, 2, 1), (1, -2, 0, -3, 0), (1, -1, 1, -2, 1), (2, 2, 0, 4, 0),
    (2, 2, 0, 2, 1), (2, -1, 1, -1, 0), (3, -1, 1, -2, 1), (3, 1, 1, 2, 1), (3, -3, 0, 4, 0), (3, -3, 0, -2, 0),
    (3, -3, 0, -3, 1), (0, -2, 1, -3, 1), (0, -1, 0, -1, 1), (1, 2, 1, 4, 1), (1, 2, 1, 1, 1), (1, 2, 1, 3, 1),
    (0, 3, 0, 3, 1), (0, 4, 0, -3, 0), (0, 4, 0, 4, 1), (2, -2, 1, -3, 1), (1, -3, 0, 4, 0), (1, -3, 0, -3, 1),
    (2, 2, 1, 3, 1), (3, 2, 1, 3, 1), (2, 4, 0, 3, 0), (2, 4, 0, 4, 1), (3, 4, 0, 3, 0), (3, 4, 0, 4, 1),
]
ARRIVALS = [
    (0, 0, 1), (0, 1, 0), (1, -1, 0), (2, 0, 1), (2, 1, 0), (3, -1, 0), (3, 0, 1), (3, 1, 0),
    (1, 0, 1), (0, -2, 0), (1, 1, 0), (1, 2, 0), (2, -2, 0), (0, 2, 0), (1, -2, 0), (1, -1, 1),
    (0, 1, 1), (2, 2, 0), (2, -1, 1), (3, -1, 1), (3, 1, 1), (2, 1, 1), (3, -3, 0), (3, 2, 0),
    (0, -2, 1), (0, -1, 0), (1, 2, 1), (1, 3, 0), (2, -3, 0), (0, 3, 0), (0, 4, 0), (2, -2, 1),
    (0, 2, 1), (1, -3, 0), (1, -2, 1), (2, 2, 1), (3, 2, 1), (2, -1, 0), (2, 4, 0), (3, -2, 1),
    (3, -3, 1), (3, -2, 0), (3, 4, 0), (0, -3, 1), (0, -1, 1), (0, 4, 1), (1, 1, 1), (1, 3, 1),
    (0, -3, 0), (0, 3, 1), (2, -3, 1), (1, -3, 1), (1, 4, 0), (1, 4, 1), (2, 3, 0), (2, 3, 1),
    (2, 4, 1), (3, 3, 0), (3, 3, 1), (3, 4, 1),
]


def tables():
    rho = np.arange(256)
    kg = rho % G
    part = (rho // G) % 2
    kp = (rho // (2 * G)) % V
    band = rho // 16
    bins = band * 8 + kp * G + kg + 1
    phase = ((np.arange(NT)[None, :] * bins[:, None]) % NT).astype(np.float64) * (2.0 * math.pi / NT)
    table = np.where(part[:, None] == 0, np.cos(phase), -np.sin(phase)).astype(np.float32)
    return jnp.asarray(table, dtype=BF16), jnp.asarray((table * (2.0 / NT)).T, dtype=BF16)


def scoped(function):
    def wrapped(*args):
        with jax.named_scope(function.__name__):
            return function(*args)
    return wrapped


def lane_bit(shape, stride):
    lanes = lax.broadcasted_iota(jnp.int32, shape, len(shape) - 1)
    return (lanes // stride) % 2 == 0


def exchange(arrays):
    shape = arrays[0].shape
    stride, span = 2 * G, 1
    while span < V:
        low = lane_bit(shape, stride)
        out = list(arrays)
        for i in range(V):
            if (i // span) % 2 == 0:
                first, second = arrays[i], arrays[i + span]
                out[i] = jnp.where(low, first, pltpu.roll(second, stride, 1))
                out[i + span] = jnp.where(low, pltpu.roll(first, 128 - stride, 1), second)
        arrays = out
        stride, span = stride * 2, span * 2
    return arrays


def kernel(
    resp, direct, onset, fwd, inv, up_out, coda_out,
    rs, x, sf, rf, sb, rb, dt, fb, prod, limits,
    r_sem, af_s, af_r, ab_s, ab_r, m_s, m_r,
):
    f = lax.axis_index("freq")
    p = lax.axis_index("rec")
    a, z, q = p // 16, (p // 2) % NZ, p % 2

    def dev(df=0, dz=0, dq=0, da=0):
        return ((f + df) % NFD, ((a + da) % 2) * 16 + ((z + dz + NZ) % NZ) * 2 + (q + dq) % 2)

    def row(a_, z_):
        return pl.multiple_of((a_ * NZ + z_) * 112, 16)

    peers = [dev(dz=1), dev(dz=-1), dev(dz=2), dev(dz=-2), dev(da=1)]
    freq_peers = [(df, dq) for df in (5, 3, 7, 1, 4, 2, 6, 0) for dq in range(2) if df or dq]

    own_r = pltpu.make_async_copy(resp.at[pl.ds(q * 8, 8)], rs.at[:, q], r_sem.at[0])
    own_r.start()

    barrier = pltpu.get_barrier_semaphore()
    for peer in peers + [dev(df=df, dq=dq) for df, dq in freq_peers]:
        pl.semaphore_signal(barrier, inc=1, device_id=peer, device_id_type=MESH)
    other_r = pltpu.make_async_remote_copy(
        src_ref=resp.at[pl.ds((1 - q) * 8, 8)], dst_ref=rs.at[:, q],
        send_sem=r_sem.at[1], recv_sem=r_sem.at[2], device_id=dev(dq=1), device_id_type=MESH)

    def spread(src_slot, dst, dst_slot, sends, recvs, ch):
        return [
            pltpu.make_async_remote_copy(
                src_ref=src_slot((f + df) % NFD, (q + dq) % 2), dst_ref=dst_slot(dst),
                send_sem=sends.at[ch, 2 * df + dq], recv_sem=recvs.at[ch, 2 * df + dq],
                device_id=dev(df=df, dq=dq), device_id_type=MESH)
            for df, dq in freq_peers]

    def sf_slot(ch):
        return lambda fd, qd: sf.at[ch, pl.ds(pl.multiple_of((fd * 2 + qd) * 16, 16), 16)]

    def sb_slot(ch):
        return lambda fd, qd: sb.at[ch, qd, pl.ds(pl.multiple_of(fd * 16, 16), 16)]

    def forward_copies(ch):
        return spread(sf_slot(ch), rf, lambda d: d.at[ch, q, pl.ds(pl.multiple_of(f * 16, 16), 16)], af_s, af_r, ch)

    def back_copies(ch):
        return spread(sb_slot(ch), rb, lambda d: d.at[ch, pl.ds(pl.multiple_of((f * 2 + q) * 16, 16), 16)],
                      ab_s, ab_r, ch)

    @scoped
    def analyse(ch, field, ready=None):
        sf[ch] = jnp.dot(fwd[...], field.astype(BF16), preferred_element_type=F32).astype(BF16)
        if ready is not None:
            ready()
        for copy in forward_copies(ch):
            copy.start()
        rf[ch, q, pl.ds(pl.multiple_of(f * 16, 16), 16)] = sf[ch, pl.ds(pl.multiple_of((f * 2 + q) * 16, 16), 16)]

    @scoped
    def collect(ch, par):
        for copy in forward_copies(ch):
            copy.wait_recv()
        for copy in forward_copies(ch):
            copy.wait_send()
        halves = []
        for core in range(2):
            parts = []
            for pair in range(V // 2):
                block = rf[ch, core, :, pair * 128:(pair + 1) * 128].astype(F32).T
                parts += [block[0:ROWS], block[ROWS:2 * ROWS]]
            halves.append(exchange(parts))
        for kp in range(V):
            x[par, ch, kp, pl.ds(row(a, z), 112), :] = jnp.concatenate(
                [halves[0][kp], halves[1][kp]], axis=0).astype(BF16)

    def message(ch, par, index, arriving=False):
        kp, d0, l0, d1, l1 = SENDS[index]
        dz, da = (d1 - d0 + 3) % NZ - 3, l1 - l0
        d, l = (d1, l1) if arriving else (d0, l0)
        ref = x.at[par, ch, kp, pl.ds(row((a + l) % 2, (z - d + NZ) % NZ), 112)]
        return pltpu.make_async_remote_copy(
            src_ref=ref, dst_ref=ref, send_sem=m_s.at[ch, index], recv_sem=m_r.at[par, ch, index],
            device_id=dev(dz=dz, da=da), device_id_type=MESH)

    def send_from(ch, par, kp, d, l):
        for index, (group, d0, l0, _, _) in enumerate(SENDS):
            if (d0, l0) == (d, l) and kp in (None, group):
                message(ch, par, index).start()

    @scoped
    def ring_start(ch, par):
        send_from(ch, par, None, 0, 0)

    def relay(ch, par, kp, d, l):
        index = [s[0:1] + s[3:5] for s in SENDS].index((kp, d, l))
        message(ch, par, index, arriving=True).wait_recv()
        send_from(ch, par, kp, d, l)

    @scoped
    def ring_drain(ch, par):
        for index in range(len(SENDS)):
            message(ch, par, index).wait_send()

    @scoped
    def apply(ch, par, n):
        sign = jnp.where(n % 2 == 0, 1.0, -1.0).astype(F32)
        shape = (ROWS, 128)
        low = lane_bit(shape, G)
        lanes = lax.broadcasted_iota(jnp.int32, shape, 1)
        groups = [[], []]
        last = {kp: place for place, (kp, _, _) in enumerate(ARRIVALS)}
        done = 0
        for kp in sorted(range(V), key=last.get):
            with jax.named_scope("gather%d" % kp):
                for each in ARRIVALS[done:last[kp] + 1]:
                    relay(ch, par, *each)
                done = last[kp] + 1
            if not groups[0]:
                @pl.when(n == 0)
                def _():
                    own_r.wait()
                    other_r.wait()
            for part in range(2):
                first = kp * G + part * (G // 2)
                prod[pl.ds(part * G * 112, G * 112), :] = jnp.dot(
                    rs[first:first + G // 2].reshape(G * 112, NS), x[par, ch, kp], preferred_element_type=F32)
            for core in range(2):
                re = im = None
                for kg in range(G):
                    base = kg * 224 + core * 112
                    re_k, im_k = prod[base:base + ROWS, :], prod[base + ROWS:base + 2 * ROWS, :]
                    mine = lanes % G == kg
                    re = re_k if re is None else jnp.where(mine, re_k, re)
                    im = im_k if im is None else jnp.where(mine, im_k, im)
                turned = jnp.where(low, -pltpu.roll(im, 128 - G, 1), pltpu.roll(im, G, 1))
                groups[core].append((kp, re + sign * turned))
        for core in range(2):
            parts = exchange([group for _, group in sorted(groups[core], key=lambda g: g[0])])
            for pair in range(V // 2):
                block = jnp.concatenate(
                    [parts[2 * pair], parts[2 * pair + 1], jnp.zeros((16, 128), F32)], axis=0)
                sb[ch, core, :, pair * 128:(pair + 1) * 128] = block.T.astype(BF16)
        for copy in back_copies(ch):
            copy.start()
        rb[ch, pl.ds(pl.multiple_of((f * 2 + q) * 16, 16), 16)] = sb[ch, q, pl.ds(pl.multiple_of(f * 16, 16), 16)]

    @scoped
    def synthesise(ch, n):
        for copy in back_copies(ch):
            copy.wait_recv()
        for copy in back_copies(ch):
            copy.wait_send()
        t = lax.broadcasted_iota(jnp.int32, (NT, LC), 0)
        inside = jnp.minimum(t, NT - t).astype(F32) < limits[0:1, ch * LC:(ch + 1) * LC]
        field = jnp.where(inside, jnp.dot(inv[...], rb[ch], preferred_element_type=F32), 0.0)
        fb[n % 2, ch] = field
        return field

    lanes8 = lax.broadcasted_iota(jnp.int32, (8, 128), 1)
    turned = jnp.concatenate([onset[...].astype(F32), jnp.zeros((NVD, 128 - ROWS), F32)], axis=1)
    for pair in range(2):
        first, second = (jnp.broadcast_to(turned[2 * pair + i:2 * pair + i + 1], (8, 128)) for i in range(2))
        limits[:, pair * 128:(pair + 1) * 128] = jnp.where(lanes8 < ROWS, first, pltpu.roll(second, ROWS, 1))
    for ch in range(CHUNKS):
        for pair in range(V // 2):
            first = ch * V + 2 * pair
            block = jnp.concatenate(
                [direct[:, first, :], direct[:, first + 1, :],
                 jnp.zeros((16, NT), F32)], axis=0)
            dt[ch, :, pair * 128:(pair + 1) * 128] = block.T
        analyse(ch, dt[ch], None if ch else lambda: pl.semaphore_wait(barrier, len(peers) + len(freq_peers)))
    collect(0, 0)
    ring_start(0, 0)
    other_r.start()

    def step(n, carry):
        par = n % 2
        apply(0, par, n)
        ring_drain(0, par)
        field = synthesise(0, n)

        @pl.when(n < 2 * ITERS - 1)
        def _():
            analyse(0, jnp.where(n % 2 == 0, field, field + dt[0]))
            collect(0, 1 - par)
            ring_start(0, 1 - par)
        return carry

    lax.fori_loop(0, 2 * ITERS, step, 0)

    for part, out in ((0, up_out), (1, coda_out)):
        for ch in range(CHUNKS):
            for pair in range(V // 2):
                block = fb[part, ch, :, pair * 128:(pair + 1) * 128].T
                for half in range(2):
                    v = ch * V + 2 * pair + half
                    out[:, v, :] = block[half * ROWS:(half + 1) * ROWS]


def body(response, direct, onset):
    fwd, inv = tables()
    vmem = pl.BlockSpec(memory_space=pltpu.VMEM)
    dma = pltpu.SemaphoreType.DMA
    return pl.pallas_call(
        kernel,
        name="marchenko",
        out_shape=[jax.ShapeDtypeStruct((ROWS, NVD, NT), F32)] * 2,
        in_specs=[pl.BlockSpec(memory_space=pl.ANY), vmem, vmem, vmem, vmem],
        out_specs=[vmem, vmem],
        scratch_shapes=[
            pltpu.VMEM((8, 2, 112, NS), BF16),
            pltpu.VMEM((2, CHUNKS, V, NS, 128), BF16),
            pltpu.VMEM((CHUNKS, 256, LC), BF16),
            pltpu.VMEM((CHUNKS, 2, 128, LC), BF16),
            pltpu.VMEM((CHUNKS, 2, 128, LC), BF16),
            pltpu.VMEM((CHUNKS, 256, LC), BF16),
            pltpu.VMEM((CHUNKS, NT, LC), F32),
            pltpu.VMEM((2, CHUNKS, NT, LC), F32),
            pltpu.VMEM((G * 224, 128), F32),
            pltpu.VMEM((8, 256), F32),
            dma((3,)),
            dma((CHUNKS, 16)), dma((CHUNKS, 16)), dma((CHUNKS, 16)), dma((CHUNKS, 16)),
            dma((CHUNKS, len(SENDS))), dma((2, CHUNKS, len(SENDS))),
        ],
        compiler_params=pltpu.CompilerParams(
            collective_id=0, has_side_effects=True, vmem_limit_bytes=60 * 2**20),
    )(response.reshape(16, 112, NS), direct, onset.T, fwd, inv)


def solution(mesh):
    placed = (P("freq", None, "rec", None), P("rec", "freq", None), P("rec", "freq"))
    return jax.shard_map(
        body, mesh=mesh, in_specs=placed,
        out_specs=(P("rec", "freq", None), P("rec", "freq", None)), check_vma=False)
```

time: 156 us -> 136 us (0.87)
  Pallas kernels: 148 us -> 132 us
  local copies, waits for them, and re-layouts: 6.46 us -> 3.28 us
    pallas_call x1, Pallas kernels: 148 us -> 132 us  [body(): pl.pallas_call(kernel, name='marchenko', out_shape=[jax.ShapeDtypeStruct(...]
    reshape x3 -> x0, local copies, waits for them, and re-layouts: 4.22 us -> none  [the longest x2 3.46 us: body(): return (up.reshape(ROWS, NVD, NT), coda.reshape(ROWS, NVD, NT))]
    unnamed x1 -> x2, local copies, waits for them, and re-layouts: 1.67 us -> 3.28 us
where the time goes in v2:
time: 136 us
  Pallas kernels  132 us (97%)
  local copies, waits for them, and re-layouts  3.28 us (2%)
    pallas_call x1, Pallas kernels, body(): pl.pallas_call(kernel, name='marchenko', out_shape=[jax.ShapeDtypeStruct(...  132 us
    unnamed x2, local copies, waits for them, and re-layouts  3.28 us

profile of v2, /device:TPU:1, one launch (start us, length us, event | category | flops | bytes accessed | tf_op | source)
XLA Modules:
  0.0 136.2 jit_solution(12607036089279443382)
XLA Ops:
  0.6 132.3 %marchenko.1 = (f32[56,4,256]{2,1,0:T(4,128)}, f32[56,4,256]{2,1,0:T(4,128)}) custom-call(bf16[16,112,1792]{2,1,0:T(8,128)(2,1)} %bitcast.2, f32[56,4,256]{2,1,0:T(4,128)} %direct.1, s32[4,56]{1,0:T(4,128)} %bitcast.3, bf16[256,256]{1,0:T(8,128)(2,1)} %constant.4.clone.fwd, bf16[256,256]{1,0:T(8,128)(2,1)} %constant.5.clone.inv), custom_call_target="tpu_custom_call" | custom-call | tf_op jit(solution)/shard_map/marchenko/pallas_call | solution.py:287
  132.9 1.6 %copy.9 = f32[56,4,256]{2,1,0:T(4,128)} copy(f32[56,4,256]{2,1,0:T(4,128)} %get-tuple-element.4) | data formatting | bytes 458752
  134.6 1.6 %copy.10 = f32[56,4,256]{2,1,0:T(4,128)} copy(f32[56,4,256]{2,1,0:T(4,128)} %get-tuple-element.5) | data formatting | bytes 458752

commit v3 on v2

--- a/solution.py
+++ b/solution.py
@@ -17,29 +17,29 @@
 LC = 64 * V
 MESH = pl.DeviceIdType.MESH
 F32, BF16 = jnp.float32, jnp.bfloat16
+EARLY = [1, 3]
 SENDS = [
-    (1, 0, 0, -1, 0), (3, 0, 0, -1, 0), (0, 0, 0, 1, 0), (0, 0, 0, 0, 1), (0, 0, 0, -2, 0), (2, 0, 0, 1, 0),
-    (2, 0, 0, 0, 1), (3, 0, 0, 0, 1), (1, 0, 0, 0, 1), (3, 0, 0, 1, 0), (1, 0, 0, 2, 0), (2, 0, 0, -2, 0),
-    (1, 0, 0, 1, 0), (0, 1, 0, 2, 0), (0, 1, 0, 1, 1), (1, -1, 0, -2, 0), (1, -1, 0, -1, 1), (2, 0, 1, -1, 1),
-    (2, 1, 0, 2, 0), (2, 1, 0, 1, 1), (3, -1, 0, -3, 0), (3, -1, 0, -1, 1), (3, 0, 1, 1, 1), (3, 1, 0, 2, 0),
-    (0, -2, 0, 4, 0), (0, -2, 0, -1, 0), (0, -2, 0, -2, 1), (1, 2, 0, 2, 1), (1, 2, 0, 3, 0), (2, -2, 0, -2, 1),
-    (2, -2, 0, -3, 0), (0, 2, 0, 3, 0), (0, 2, 0, 2, 1), (1, -2, 0, -3, 0), (1, -1, 1, -2, 1), (2, 2, 0, 4, 0),
-    (2, 2, 0, 2, 1), (2, -1, 1, -1, 0), (3, -1, 1, -2, 1), (3, 1, 1, 2, 1), (3, -3, 0, 4, 0), (3, -3, 0, -2, 0),
-    (3, -3, 0, -3, 1), (0, -2, 1, -3, 1), (0, -1, 0, -1, 1), (1, 2, 1, 4, 1), (1, 2, 1, 1, 1), (1, 2, 1, 3, 1),
-    (0, 3, 0, 3, 1), (0, 4, 0, -3, 0), (0, 4, 0, 4, 1), (2, -2, 1, -3, 1), (1, -3, 0, 4, 0), (1, -3, 0, -3, 1),
-    (2, 2, 1, 3, 1), (3, 2, 1, 3, 1), (2, 4, 0, 3, 0), (2, 4, 0, 4, 1), (3, 4, 0, 3, 0), (3, 4, 0, 4, 1),
+    (3, 0, 0, 1, 0), (2, 0, 0, 1, 0), (0, 0, 0, -1, 0), (0, 0, 0, 1, 0), (0, 0, 0, 0, 1), (1, 0, 0, 0, 1),
+    (2, 0, 0, -1, 0), (3, 0, 0, -2, 0), (1, 0, 0, 1, 0), (1, 0, 0, -2, 0), (2, 0, 0, 0, 1), (0, 0, 0, 2, 0),
+    (3, 0, 0, 0, 1), (0, -1, 0, -1, 1), (0, -1, 0, -2, 0), (0, 2, 0, 3, 0), (0, 2, 0, 2, 1), (0, -3, 1, 4, 1),
+    (0, -3, 1, -3, 0), (0, 3, 0, 4, 0), (0, 3, 0, 3, 1), (0, 1, 0, 1, 1), (0, -1, 1, -3, 1), (0, -1, 1, -2, 1),
+    (1, 1, 0, 2, 0), (1, 1, 0, 1, 1), (1, -2, 0, -1, 0), (1, -2, 0, -3, 0), (1, -2, 0, -2, 1), (1, -1, 0, -1, 1),
+    (1, 2, 0, 3, 0), (1, -3, 0, 4, 0), (1, -3, 0, -3, 1), (1, 0, 1, 2, 1), (1, 2, 1, 4, 1), (1, 2, 1, 3, 1),
+    (2, 1, 0, 2, 0), (2, -1, 0, -3, 0), (2, -1, 0, -2, 0), (2, -1, 0, -1, 1), (2, 4, 0, 3, 0), (2, 4, 0, 4, 1),
+    (2, -3, 0, 4, 0), (2, -3, 0, -3, 1), (2, 2, 1, 1, 1), (2, 2, 1, 3, 1), (2, 2, 0, 2, 1), (2, -2, 0, -2, 1),
+    (3, -2, 0, 4, 0), (3, -2, 0, -1, 0), (3, -2, 0, -2, 1), (3, -2, 0, -3, 0), (3, 1, 0, 2, 0), (3, 2, 0, 2, 1),
+    (3, 2, 0, 3, 0), (3, 2, 1, 1, 1), (3, 2, 1, 3, 1), (3, -1, 0, -1, 1), (3, -2, 1, -3, 1), (3, 4, 0, 4, 1),
 ]
 ARRIVALS = [
-    (0, 0, 1), (0, 1, 0), (1, -1, 0), (2, 0, 1), (2, 1, 0), (3, -1, 0), (3, 0, 1), (3, 1, 0),
-    (1, 0, 1), (0, -2, 0), (1, 1, 0), (1, 2, 0), (2, -2, 0), (0, 2, 0), (1, -2, 0), (1, -1, 1),
-    (0, 1, 1), (2, 2, 0), (2, -1, 1), (3, -1, 1), (3, 1, 1), (2, 1, 1), (3, -3, 0), (3, 2, 0),
-    (0, -2, 1), (0, -1, 0), (1, 2, 1), (1, 3, 0), (2, -3, 0), (0, 3, 0), (0, 4, 0), (2, -2, 1),
-    (0, 2, 1), (1, -3, 0), (1, -2, 1), (2, 2, 1), (3, 2, 1), (2, -1, 0), (2, 4, 0), (3, -2, 1),
-    (3, -3, 1), (3, -2, 0), (3, 4, 0), (0, -3, 1), (0, -1, 1), (0, 4, 1), (1, 1, 1), (1, 3, 1),
-    (0, -3, 0), (0, 3, 1), (2, -3, 1), (1, -3, 1), (1, 4, 0), (1, 4, 1), (2, 3, 0), (2, 3, 1),
-    (2, 4, 1), (3, 3, 0), (3, 3, 1), (3, 4, 1),
+    (3, 1, 0), (0, -1, 0), (0, 0, 1), (2, 1, 0), (2, -1, 0), (1, 0, 1), (0, 1, 0), (2, 0, 1),
+    (1, 1, 0), (3, 0, 1), (3, -2, 0), (1, -2, 0), (0, 2, 0), (3, 2, 0), (0, -2, 0), (0, -1, 1),
+    (2, 2, 0), (2, -1, 1), (0, 1, 1), (2, -2, 0), (2, -3, 0), (1, 1, 1), (1, 2, 0), (1, 2, 1),
+    (3, -2, 1), (3, -1, 0), (1, -2, 1), (1, -1, 0), (3, -3, 0), (0, 2, 1), (3, 4, 0), (0, 3, 0),
+    (1, -3, 0), (3, 2, 1), (3, 3, 0), (2, 2, 1), (2, -2, 1), (1, 3, 0), (0, -2, 1), (2, -3, 1),
+    (0, -3, 1), (2, 4, 0), (3, -1, 1), (3, -3, 1), (1, -1, 1), (1, 3, 1), (1, 4, 1), (3, 4, 1),
+    (1, 4, 0), (0, 4, 0), (0, 3, 1), (3, 1, 1), (3, 3, 1), (1, -3, 1), (2, 1, 1), (2, 3, 1),
+    (0, 4, 1), (0, -3, 0), (2, 3, 0), (2, 4, 1),
 ]
-
 
 def tables():
     rho = np.arange(256)
@@ -82,8 +82,8 @@
 
 
 def kernel(
-    resp, direct, onset, fwd, inv, up_out, coda_out,
-    rs, x, sf, rf, sb, rb, dt, fb, prod, limits,
+    resp, direct_in, onset_in, fwd_in, inv_in, fields,
+    direct, onset, fwd, inv, fb, rs, x, sf, rf, sb, rb, dt, prod, limits, in_sem, out_sem,
     r_sem, af_s, af_r, ab_s, ab_r, m_s, m_r,
 ):
     f = lax.axis_index("freq")
@@ -98,9 +98,6 @@
 
     peers = [dev(dz=1), dev(dz=-1), dev(dz=2), dev(dz=-2), dev(da=1)]
     freq_peers = [(df, dq) for df in (5, 3, 7, 1, 4, 2, 6, 0) for dq in range(2) if df or dq]
-
-    own_r = pltpu.make_async_copy(resp.at[pl.ds(q * 8, 8)], rs.at[:, q], r_sem.at[0])
-    own_r.start()
 
     barrier = pltpu.get_barrier_semaphore()
     for peer in peers + [dev(df=df, dq=dq) for df, dq in freq_peers]:
@@ -108,6 +105,19 @@
     other_r = pltpu.make_async_remote_copy(
         src_ref=resp.at[pl.ds((1 - q) * 8, 8)], dst_ref=rs.at[:, q],
         send_sem=r_sem.at[1], recv_sem=r_sem.at[2], device_id=dev(dq=1), device_id_type=MESH)
+
+    inputs = [
+        pltpu.make_async_copy(source, held, in_sem.at[place]) for place, (source, held) in enumerate(
+            ((onset_in, onset), (direct_in, direct), (fwd_in, fwd), (inv_in, inv)))]
+    for copy in inputs:
+        copy.start()
+    own_r = pltpu.make_async_copy(resp.at[pl.ds(q * 8, 8)], rs.at[:, q], r_sem.at[0])
+    own_r.start()
+    for copy in inputs:
+        copy.wait()
+
+    def result(part):
+        return pltpu.make_async_copy(fb.at[part], fields.at[part], out_sem.at[part])
 
     def spread(src_slot, dst, dst_slot, sends, recvs, ch):
         return [
@@ -191,22 +201,26 @@
         low = lane_bit(shape, G)
         lanes = lax.broadcasted_iota(jnp.int32, shape, 1)
         groups = [[], []]
-        last = {kp: place for place, (kp, _, _) in enumerate(ARRIVALS)}
-        done = 0
-        for kp in sorted(range(V), key=last.get):
-            with jax.named_scope("gather%d" % kp):
-                for each in ARRIVALS[done:last[kp] + 1]:
-                    relay(ch, par, *each)
-                done = last[kp] + 1
-            if not groups[0]:
-                @pl.when(n == 0)
-                def _():
-                    own_r.wait()
-                    other_r.wait()
-            for part in range(2):
-                first = kp * G + part * (G // 2)
-                prod[pl.ds(part * G * 112, G * 112), :] = jnp.dot(
-                    rs[first:first + G // 2].reshape(G * 112, NS), x[par, ch, kp], preferred_element_type=F32)
+        holders = {(kp, d, l) for kp, d, l, _, _ in SENDS}
+        relays = [each for each in ARRIVALS if each in holders]
+        leaves = [each for each in ARRIVALS if each not in holders]
+        with jax.named_scope("gather"):
+            for each in relays + [each for each in leaves if each[0] in EARLY]:
+                relay(ch, par, *each)
+
+        @pl.when(n == 0)
+        def _():
+            own_r.wait()
+            other_r.wait()
+
+        for kp in EARLY + [kp for kp in range(V) if kp not in EARLY]:
+            if kp not in EARLY and len(groups[0]) == len(EARLY):
+                with jax.named_scope("gather_late"):
+                    for each in leaves:
+                        if each[0] not in EARLY:
+                            relay(ch, par, *each)
+            prod[...] = jnp.dot(
+                rs[kp * G:(kp + 1) * G].reshape(G * 224, NS), x[par, ch, kp], preferred_element_type=F32)
             for core in range(2):
                 re = im = None
                 for kg in range(G):
@@ -264,33 +278,46 @@
 
         @pl.when(n < 2 * ITERS - 1)
         def _():
+            @pl.when(n == 2 * ITERS - 2)
+            def _():
+                result(0).start()
+
             analyse(0, jnp.where(n % 2 == 0, field, field + dt[0]))
             collect(0, 1 - par)
             ring_start(0, 1 - par)
         return carry
 
     lax.fori_loop(0, 2 * ITERS, step, 0)
-
+    result(1).start()
+    result(0).wait()
+    result(1).wait()
+
+
+def turn(fields, up_out, coda_out):
     for part, out in ((0, up_out), (1, coda_out)):
         for ch in range(CHUNKS):
             for pair in range(V // 2):
-                block = fb[part, ch, :, pair * 128:(pair + 1) * 128].T
+                block = fields[part, ch, :, pair * 128:(pair + 1) * 128].T
                 for half in range(2):
-                    v = ch * V + 2 * pair + half
-                    out[:, v, :] = block[half * ROWS:(half + 1) * ROWS]
+                    out[:, ch * V + 2 * pair + half, :] = block[half * ROWS:(half + 1) * ROWS]
 
 
 def body(response, direct, onset):
     fwd, inv = tables()
-    vmem = pl.BlockSpec(memory_space=pltpu.VMEM)
+    vmem, hbm = pl.BlockSpec(memory_space=pltpu.VMEM), pl.BlockSpec(memory_space=pltpu.HBM)
     dma = pltpu.SemaphoreType.DMA
-    return pl.pallas_call(
+    fields = pl.pallas_call(
         kernel,
         name="marchenko",
-        out_shape=[jax.ShapeDtypeStruct((ROWS, NVD, NT), F32)] * 2,
-        in_specs=[pl.BlockSpec(memory_space=pl.ANY), vmem, vmem, vmem, vmem],
-        out_specs=[vmem, vmem],
+        out_shape=jax.ShapeDtypeStruct((2, CHUNKS, NT, LC), F32),
+        in_specs=[hbm] * 5,
+        out_specs=hbm,
         scratch_shapes=[
+            pltpu.VMEM((ROWS, NVD, NT), F32),
+            pltpu.VMEM((NVD, ROWS), jnp.int32),
+            pltpu.VMEM((256, NT), BF16),
+            pltpu.VMEM((NT, 256), BF16),
+            pltpu.VMEM((2, CHUNKS, NT, LC), F32),
             pltpu.VMEM((8, 2, 112, NS), BF16),
             pltpu.VMEM((2, CHUNKS, V, NS, 128), BF16),
             pltpu.VMEM((CHUNKS, 256, LC), BF16),
@@ -298,16 +325,24 @@
             pltpu.VMEM((CHUNKS, 2, 128, LC), BF16),
             pltpu.VMEM((CHUNKS, 256, LC), BF16),
             pltpu.VMEM((CHUNKS, NT, LC), F32),
-            pltpu.VMEM((2, CHUNKS, NT, LC), F32),
             pltpu.VMEM((G * 224, 128), F32),
             pltpu.VMEM((8, 256), F32),
+            dma((4,)), dma((2,)),
             dma((3,)),
             dma((CHUNKS, 16)), dma((CHUNKS, 16)), dma((CHUNKS, 16)), dma((CHUNKS, 16)),
             dma((CHUNKS, len(SENDS))), dma((2, CHUNKS, len(SENDS))),
         ],
         compiler_params=pltpu.CompilerParams(
-            collective_id=0, has_side_effects=True, vmem_limit_bytes=60 * 2**20),
+            collective_id=0, has_side_effects=True, vmem_limit_bytes=58 * 2**20),
     )(response.reshape(16, 112, NS), direct, onset.T, fwd, inv)
+    return pl.pallas_call(
+        turn,
+        name="turn",
+        out_shape=[jax.ShapeDtypeStruct((ROWS, NVD, NT), F32)] * 2,
+        in_specs=[vmem],
+        out_specs=[vmem, vmem],
+        compiler_params=pltpu.CompilerParams(vmem_limit_bytes=8 * 2**20),
+    )(fields)
 
 
 def solution(mesh):

time: 136 us -> 133 us (0.978)
  local copies, waits for them, and re-layouts: 3.28 us -> 1.03 us
    unnamed x2, local copies, waits for them, and re-layouts: 3.28 us -> 1.03 us
    pallas_call x1 -> x2, Pallas kernels: 132 us -> 131 us  [the longest x1 130 us: body(): pl.pallas_call(kernel, name='marchenko', out_shape=jax.ShapeDtypeStruct((...]
where the time goes in v3:
time: 133 us
  Pallas kernels  131 us (98%)
    pallas_call x1, Pallas kernels, body(): pl.pallas_call(kernel, name='marchenko', out_shape=jax.ShapeDtypeStruct((...  130 us

profile of v3, /device:TPU:1, one launch (start us, length us, event | category | flops | bytes accessed | tf_op | source)
XLA Modules:
  0.0 133.0 jit_solution(880850622098163774)
XLA Ops:
  0.6 130.4 %marchenko.1.fields = f32[2,1,256,256]{3,2,1,0:T(8,128)} custom-call(bf16[16,112,1792]{2,1,0:T(8,128)(2,1)} %bitcast.2, f32[56,4,256]{2,1,0:T(4,128)} %direct_in.1, s32[4,56]{1,0:T(4,128)} %bitcast.3, bf16[256,256]{1,0:T(8,128)(2,1)} %constant.4.clone.fwd_in, bf16[256,256]{1,0:T(8,128)(2,1)} %constant.5.clone.inv_in), custom_call_target="tpu_custom_call" | custom-call | tf_op jit(solution)/shard_map/marchenko/pallas_call | solution.py:309
  131.1 0.0 copy-start
  131.1 1.0 copy-done
  132.1 0.9 turn.1
Async XLA Ops:
  131.1 1.0 copy-start
